TPU v7x, 32 devices: a whole 2x2x4 slice. The times are simulated.
32 devices in a mesh: grp: 4 (over x, core), seq: 8 (over z, y).
Axes of the slice: x: 2, y: 2, z: 4, core: 2. Of those that a mesh axis runs over, the one named last changes fastest.
Arguments:
- patches: bfloat16 [2048, 1280], P(('grp', 'seq')), may hold values from -60 to 60
- piece_ids: int32 [32, 64], P(('grp', 'seq')), may hold values from 0 to 2, never falling along the last dimension, each value on 1 to 48 neighbouring positions
- vit_gain: float32 [1280], replicated, may hold values from 0.25 to 1.75
- vit_qkv: bfloat16 [1280, 3840], replicated
- vit_out: bfloat16 [1280, 1280], replicated, may hold values from -0.15625 to 0.15625
- merge_gain: float32 [1280], replicated, may hold values from 0.25 to 1.75
- merge_up: bfloat16 [5120, 5120], P(None, 'seq'), may hold values from -0.078125 to 0.078125
- merge_down: bfloat16 [5120, 8192], P(None, 'seq'), may hold values from -0.078125 to 0.078125
- dest: int32 [512], P(('grp', 'seq')), may hold values from 0 to 7, as said below
- tokens: bfloat16 [8192, 8192], P(('grp', 'seq')), may hold values from -60 to 60
- image_index: int32 [8192], P(('grp', 'seq')), may hold values from 0 to 32, as said below
- doc_lengths: int32 [4, 4], P('grp'), may hold values from 1 to 1024, 2048 in all within a row
- attn_gain: float32 [8192], replicated, may hold values from 0.25 to 1.75
- attn_qkv: bfloat16 [8192, 768], P(('grp', 'seq'))
- attn_out: bfloat16 [512, 8192], P(None, ('grp', 'seq')), may hold values from -0.25 to 0.25
Outputs:
- layer_out: bfloat16 [8192, 8192], P(('grp', 'seq'))
Inputs may be any that keep to these rules, and one draw needn't show every extreme that they name: `dest`: within each aligned block of 16 rows (one device's merged rows), exactly 4 distinct values occur, each exactly 4 times, and in every group one device is named by every device of the group. `image_index`: 32 marks a text token. A value k < 32 on a device names the merged row that the device of seq index k // 4 in its group sends to it as its (k % 4)-th row in row order; each such row is named by exactly one token of the receiving device, and no other values occur. `piece_ids`: piece numbers never fall within a window. `doc_lengths`: each group's documents fill its 2048 positions.
All inputs are finite; a program needn't handle non-finite values.
Results may differ from a plain program's by a relative error of at most 0.0093.
The roundings to bfloat16 on the way count: a program that leaves them out, or rounds other values in their place, can miss the bound.
Values may be sent and summed in bfloat16 or wider, within the bound.
A program may use at most 192 MiB of HBM per device.

v0:
```python
import jax
import jax.numpy as jnp
from jax import lax
from jax.sharding import PartitionSpec as P

VHEADS = 16
WIN = 64
EPSILON = 1e-06


def from_behind(value, axis, steps):
    count = lax.axis_size(axis)
    first, last = (max(0, -steps), min(count, count - steps))
    return lax.ppermute(value, axis, [(source, source + steps) for source in range(first, last)])


def rms_scale(inputs, gain):
    mean_square = jnp.mean(inputs * inputs, axis=-1, keepdims=True)
    return inputs * lax.rsqrt(mean_square + EPSILON) * gain


def softmax_mix(scores, allowed, value_collection, spec):
    scores = jnp.where(allowed[None], scores, -1e30)
    highest = jnp.max(scores, axis=-1, keepdims=True)
    weights = jnp.exp(scores - highest)
    totals = jnp.sum(weights, axis=-1)
    mixture = jnp.einsum(
        spec, weights.astype(jnp.bfloat16), value_collection, preferred_element_type=jnp.float32
    )
    return mixture / jnp.transpose(totals)[:, :, None]


def window_layer(patch_rows, piece_rows, vit_gain, vit_qkv, vit_out, merge_gain):
    row_count, features = patch_rows.shape
    head_dim = features // VHEADS
    residual = patch_rows.astype(jnp.float32)
    normed = rms_scale(residual, vit_gain).astype(jnp.bfloat16)
    projected = jnp.dot(normed, vit_qkv, preferred_element_type=jnp.float32).astype(jnp.bfloat16)
    queries = projected[:, :features].reshape(row_count, VHEADS, head_dim)
    key_set = projected[:, features : 2 * features].reshape(row_count, VHEADS, head_dim)
    value_collection = projected[:, 2 * features :].reshape(row_count, VHEADS, head_dim)
    scores = jnp.einsum(
        "qhd,khd->hqk", queries, key_set, preferred_element_type=jnp.float32
    ) * head_dim ** (-0.5)
    frames = jnp.arange(row_count, dtype=jnp.int32) // WIN
    allowed = (frames[:, None] == frames[None, :]) & (piece_rows[:, None] == piece_rows[None, :])
    mixture = softmax_mix(scores, allowed, value_collection, "hqk,khd->qhd")
    mixture = mixture.reshape(row_count, features).astype(jnp.bfloat16)
    residual = residual + jnp.dot(mixture, vit_out, preferred_element_type=jnp.float32)
    merge_input = rms_scale(residual, merge_gain).astype(jnp.bfloat16)
    return merge_input.reshape(row_count // 4, 4 * features)


def attend(query_rows, query_pos, query_start, key_value, key_pos):
    row_count = query_rows.shape[0]
    head_dim = key_value.shape[1] // 2
    heads = query_rows.shape[1] // head_dim
    queries = query_rows.reshape(row_count, heads, head_dim)
    scores = jnp.einsum(
        "qhd,kd->hqk", queries, key_value[:, :head_dim], preferred_element_type=jnp.float32
    ) * head_dim ** (-0.5)
    allowed = (key_pos[None, :] >= query_start[:, None]) & (key_pos[None, :] <= query_pos[:, None])
    mixture = softmax_mix(scores, allowed, key_value[:, head_dim:], "hqk,kd->qhd")
    return mixture.reshape(row_count, heads * head_dim).astype(jnp.bfloat16)


def slot_numbers(targets):
    row_count = targets.shape[-1]
    order = jnp.arange(row_count, dtype=jnp.int32)
    same = targets[..., :, None] == targets[..., None, :]
    earlier = order[None, :] < order[:, None]
    return jnp.sum(same & earlier, axis=-1)


def on_device(
    patches,
    piece_ids,
    vit_gain,
    vit_qkv,
    vit_out,
    merge_gain,
    merge_up,
    merge_down,
    dest,
    tokens,
    image_index,
    doc_lengths,
    attn_gain,
    attn_qkv,
    attn_out,
):
    features = patches.shape[1]
    block_len = WIN
    patch_blocks = patches.reshape(-1, block_len, features)
    merge_input = lax.map(
        lambda parts: window_layer(parts[0], parts[1], vit_gain, vit_qkv, vit_out, merge_gain),
        (patch_blocks, piece_ids),
    ).reshape(-1, 4 * features)
    own_rows = merge_input.shape[0]
    seq_count = lax.axis_size("seq")
    seq_index = lax.axis_index("seq")
    hidden_part = jax.nn.gelu(
        jnp.dot(
            lax.all_gather(merge_input, "seq", axis=0, tiled=True),
            merge_up,
            preferred_element_type=jnp.float32,
        ),
        approximate=False,
    ).astype(jnp.bfloat16)
    column_part = jnp.dot(
        lax.all_gather(hidden_part, "seq", axis=1, tiled=True),
        merge_down,
        preferred_element_type=jnp.float32,
    ).astype(jnp.bfloat16)
    capacity = own_rows // (seq_count // 2)
    slots = seq_count * capacity
    receivers = jnp.arange(seq_count, dtype=jnp.int32)
    slot_ids = jnp.arange(capacity, dtype=jnp.int32)
    home_rows = lax.all_to_all(column_part, "seq", split_axis=0, concat_axis=1, tiled=True)
    order = slot_numbers(dest)
    select = (dest[None, None, :] == receivers[:, None, None]) & (
        order[None, None, :] == slot_ids[None, :, None]
    )
    outgoing = jnp.einsum(
        "dcj,jf->dcf", select.astype(jnp.bfloat16), home_rows, preferred_element_type=jnp.float32
    ).astype(jnp.bfloat16)
    arrived = lax.all_to_all(outgoing, "seq", split_axis=0, concat_axis=0, tiled=True).reshape(
        slots, -1
    )
    slot_all = jnp.arange(slots, dtype=jnp.int32)
    picker = (image_index[:, None] == slot_all[None, :]).astype(jnp.bfloat16)
    pictured = jnp.dot(picker, arrived, preferred_element_type=jnp.float32).astype(jnp.bfloat16)
    layer_in = jnp.where((image_index < slots)[:, None], pictured, tokens)
    tok_rows = tokens.shape[0]
    normed = rms_scale(layer_in.astype(jnp.float32), attn_gain).astype(jnp.bfloat16)
    projected = jnp.dot(
        normed,
        lax.all_gather(attn_qkv, ("grp", "seq"), axis=0, tiled=True),
        preferred_element_type=jnp.float32,
    ).astype(jnp.bfloat16)
    query_width = attn_out.shape[0]
    queries = projected[:, :query_width]
    key_value = projected[:, query_width:]
    head_dim = key_value.shape[1] // 2
    head_count = query_width // head_dim
    positions = seq_index * tok_rows + jnp.arange(tok_rows, dtype=jnp.int32)
    lengths = doc_lengths[0]
    starts = jnp.cumsum(lengths) - lengths
    doc_start = jnp.max(
        jnp.where(starts[None, :] <= positions[:, None], starts[None, :], 0), axis=1
    )
    reach = seq_count // 2
    buffer = jnp.zeros(((reach + 1) * tok_rows, key_value.shape[1]), key_value.dtype)
    buffer = lax.dynamic_update_slice_in_dim(buffer, key_value, reach * tok_rows, 0)

    def step_back(turn, state):
        current, filled = state
        current = from_behind(current, "seq", 1)
        filled = lax.dynamic_update_slice_in_dim(filled, current, (reach - turn) * tok_rows, 0)
        return (current, filled)

    key_rows = lax.fori_loop(1, reach + 1, step_back, (key_value, buffer))[1]
    key_pos = (seq_index - reach) * tok_rows + jnp.arange(key_rows.shape[0], dtype=jnp.int32)
    block_rows = min(tok_rows, 512)
    head_queries = queries.reshape(tok_rows, head_count, head_dim).transpose(1, 0, 2)

    def one_head(head_rows):
        return lax.map(
            lambda parts: attend(parts[0], parts[1], parts[2], key_rows, key_pos),
            (
                head_rows.reshape(-1, block_rows, head_dim),
                positions.reshape(-1, block_rows),
                doc_start.reshape(-1, block_rows),
            ),
        ).reshape(tok_rows, head_dim)

    attended = lax.map(one_head, head_queries).transpose(1, 0, 2).reshape(tok_rows, query_width)
    update = jnp.dot(
        attended,
        lax.all_gather(attn_out, ("grp", "seq"), axis=1, tiled=True),
        preferred_element_type=jnp.float32,
    )
    return (layer_in.astype(jnp.float32) + update).astype(jnp.bfloat16)


def solution(mesh):
    placed = (
        P(("grp", "seq"), None),
        P(("grp", "seq"), None),
        P(),
        P(),
        P(),
        P(),
        P(None, "seq"),
        P(None, "seq"),
        P(("grp", "seq")),
        P(("grp", "seq"), None),
        P(("grp", "seq")),
        P("grp", None),
        P(),
        P(("grp", "seq"), None),
        P(None, ("grp", "seq")),
    )
    return jax.shard_map(
        on_device, mesh=mesh, in_specs=placed, out_specs=P(("grp", "seq"), None), check_vma=False
    )
```

profile of v0, /device:TPU:0, one launch (start us, length us, event | category | flops | bytes accessed | tf_op | source)
XLA Modules:
  0.0 336.6 jit_solution(14184736836307715326)
XLA Ops:
  6.5 1.2 fusion.36
  7.8 5.8 %convolution_convert_fusion.2 = bf16[64,3840]{1,0:T(8,128)(2,1)S(1)} fusion(bf16[1280,3840]{1,0:T(8,128)(2,1)} %param.22, bf16[64,1280]{1,0:T(8,128)(2,1)} %param.19, f32[1280]{0:T(1024)} %param.21, f32[64]{0:T(128)S(1)} %add_rsqrt_fusion.2), kind=kOutput, calls=%fused_computation.33 | convolution fusion | flops 629719040 | bytes 10491136 | tf_op jit(solution)/shard_map/while/body/eval_jaxpr/dot_general | solution.py:38
  13.6 0.8 fusion.63
  14.4 2.0 reshape.346
  16.4 2.0 reshape.347
  18.4 2.0 reshape.345
  20.5 1.3 fusion.64
  21.9 1.3 fusion.33
  23.2 0.9 copy.44
  24.1 1.9 convert_element_type.84
  26.0 1.7 multiply_reduce_fusion
  27.8 0.8 reshape.348
  28.7 44.6 %all-gather.5.cloned.1.call-done = bf16[128,5120]{1,0:T(8,128)(2,1)} async-done(((bf16[16,5120]{1,0:T(8,128)(2,1)}), bf16[128,5120]{1,0:T(8,128)(2,1)}) %all-gather.5.cloned.1.call-update) | async-done | bytes 1310736 | tf_op jit(solution)/shard_map/all_gather | solution.py:104
  73.3 5.8 %fusion.41 = bf16[128,640]{1,0:T(8,128)(2,1)} fusion(bf16[128,5120]{1,0:T(8,128)(2,1)} %all-gather.5.cloned.1.call-done, bf16[5120,640]{1,0:T(8,128)(2,1)} %param.25), kind=kOutput, calls=%fused_computation.56 | convolution fusion | flops 844185600 | bytes 8028160 | tf_op jit(solution)/shard_map/dot_general | solution.py:103
  79.2 0.7 all-gather.9.cloned.1.call-update
  79.9 0.5 all-gather.11.cloned.1.call-update
  80.4 40.2 %all-gather.7.cloned.1.call-done = bf16[128,5120]{1,0:T(8,128)(2,1)} async-done(((bf16[128,640]{1,0:T(8,128)(2,1)}), bf16[128,5120]{1,0:T(8,128)(2,1)}) %all-gather.7.cloned.1.call-update) | async-done | bytes 1310736 | tf_op jit(solution)/shard_map/all_gather | solution.py:111
  120.6 6.6 %convolution_convert_fusion.3 = bf16[128,1024]{1,0:T(8,128)(2,1)} fusion(bf16[128,5120]{1,0:T(8,128)(2,1)} %all-gather.7.cloned.1.call-done, bf16[5120,1024]{1,0:T(8,128)(2,1)} %param.26), kind=kOutput, calls=%fused_computation.44 | convolution fusion | flops 1342308352 | bytes 12058624 | tf_op jit(solution)/shard_map/dot_general | solution.py:110
  127.3 3.5 %all-to-all-start = ((bf16[8,16,1024]{2,1,0:T(8,128)(2,1)}), bf16[8,16,1024]{2,1,0:T(8,128)(2,1)S(1)}, u32[]{:S(2)}, u32[]{:S(2)}) async-start(bf16[8,16,1024]{2,1,0:T(8,128)(2,1)} %bitcast.3), calls=%async_computation | async-start | bytes 524288 | tf_op jit(solution)/shard_map/all_to_all | solution.py:119
  131.0 13.7 %all-to-all-done = bf16[8,16,1024]{2,1,0:T(8,128)(2,1)S(1)} async-done(((bf16[8,16,1024]{2,1,0:T(8,128)(2,1)}), bf16[8,16,1024]{2,1,0:T(8,128)(2,1)S(1)}, u32[]{:S(2)}, u32[]{:S(2)}) %all-to-all-start) | async-done | bytes 262176 | tf_op jit(solution)/shard_map/all_to_all | solution.py:119
  145.3 1.2 copy.46
  146.5 3.7 %all-to-all-start.1 = ((bf16[8,4,8192]{2,1,0:T(4,128)(2,1)}), bf16[8,4,8192]{2,1,0:T(4,128)(2,1)S(1)}, u32[]{:S(2)}, u32[]{:S(2)}) async-start(bf16[8,4,8192]{2,1,0:T(4,128)(2,1)} %copy.46), calls=%async_computation.1 | async-start | bytes 1048576 | tf_op jit(solution)/shard_map/all_to_all | solution.py:127
  150.4 25.3 %all-to-all-done.1 = bf16[8,4,8192]{2,1,0:T(4,128)(2,1)S(1)} async-done(((bf16[8,4,8192]{2,1,0:T(4,128)(2,1)}), bf16[8,4,8192]{2,1,0:T(4,128)(2,1)S(1)}, u32[]{:S(2)}, u32[]{:S(2)}) %all-to-all-start.1) | async-done | bytes 524320 | tf_op jit(solution)/shard_map/all_to_all | solution.py:127
  175.9 4.8 %fusion.21 = (f32[256]{0:T(256)S(1)}, bf16[256,8192]{1,0:T(8,128)(2,1)}) fusion(bf16[256,8192]{1,0:T(8,128)(2,1)} %param.28, bf16[32,8192]{1,0:T(8,128)(2,1)S(1)} %reshape.349, s32[256]{0:T(256)S(1)} %copy-done.6, pred[256]{0:T(512)(128)(4,1)S(1)} %broadcast_compare_fusion), kind=kOutput, calls=%fused_computation.30 | convolution fusion | flops 144711424 | bytes 8915200 | tf_op jit(solution)/shard_map/dot_general | solution.py:132
  180.7 44.7 %all-gather.9.cloned.1.call-done = bf16[8192,768]{1,0:T(8,128)(2,1)} async-done(((bf16[256,768]{1,0:T(8,128)(2,1)}), bf16[8192,768]{1,0:T(8,128)(2,1)}) %all-gather.9.cloned.1.call-update) | async-done | bytes 12582928 | tf_op jit(solution)/shard_map/all_gather | solution.py:138
  225.4 9.3 %fusion.28 = bf16[256,768]{1,0:T(8,128)(2,1)S(1)} fusion(bf16[8192,768]{1,0:T(8,128)(2,1)} %all-gather.9.cloned.1.call-done, bf16[256,8192]{1,0:T(8,128)(2,1)} %get-tuple-element.202, f32[8192]{0:T(1024)S(1)} %copy-done.5, f32[256]{0:T(256)S(1)} %add_rsqrt_fusion), kind=kOutput, calls=%fused_computation.38 | convolution fusion | flops 3229810688 | bytes 17204224 | tf_op jit(solution)/shard_map/dot_general | solution.py:136
  234.9 30.8 %while.20 = (s32[]{:T(128)}, bf16[256,256]{1,0:T(8,128)(2,1)S(1)}, bf16[1280,256]{1,0:T(8,128)(2,1)S(1)}, s32[]{:T(128)}, s32[]{:T(128)}, /*index=5*/s32[]{:T(128)}, s32[]{:T(128)}, s32[]{:T(128)}) while((s32[]{:T(128)}, bf16[256,256]{1,0:T(8,128)(2,1)S(1)}, bf16[1280,256]{1,0:T(8,128)(2,1)S(1)}, s32[]{:T(128)}, s32[]{:T(128)}, ...), condition=%wide.region_9.10_spmd, body=%wide.region_8.9_spmd.sunk | while | flops 7 | bytes 1048763 | solution.py:162
  234.9 3.4 %collective-permute-start = (bf16[256,256]{1,0:T(8,128)(2,1)S(1)}, bf16[256,256]{1,0:T(8,128)(2,1)S(1)}, u32[]{:S(2)}, u32[]{:S(2)}) collective-permute-start(bf16[256,256]{1,0:T(8,128)(2,1)S(1)} %get-tuple-element.278), channel_id=1, source_target_pairs={{0,1},{1,2},{2,3},{3,4},{4,5},{5,6},{6,7},{8,9},{9,10},{10,11},{11... | collective-permute-start | bytes 393224 | tf_op jit(solution)/shard_map/while/body/eval_jaxpr/ppermute | solution.py:14
  238.3 3.1 collective-permute-done
  241.5 4.4 %collective-permute-start = (bf16[256,256]{1,0:T(8,128)(2,1)S(1)}, bf16[256,256]{1,0:T(8,128)(2,1)S(1)}, u32[]{:S(2)}, u32[]{:S(2)}) collective-permute-start(bf16[256,256]{1,0:T(8,128)(2,1)S(1)} %get-tuple-element.278), channel_id=1, source_target_pairs={{0,1},{1,2},{2,3},{3,4},{4,5},{5,6},{6,7},{8,9},{9,10},{10,11},{11... | collective-permute-start | bytes 393224 | tf_op jit(solution)/shard_map/while/body/eval_jaxpr/ppermute | solution.py:14
  245.9 2.5 collective-permute-done
  248.4 4.5 %collective-permute-start = (bf16[256,256]{1,0:T(8,128)(2,1)S(1)}, bf16[256,256]{1,0:T(8,128)(2,1)S(1)}, u32[]{:S(2)}, u32[]{:S(2)}) collective-permute-start(bf16[256,256]{1,0:T(8,128)(2,1)S(1)} %get-tuple-element.278), channel_id=1, source_target_pairs={{0,1},{1,2},{2,3},{3,4},{4,5},{5,6},{6,7},{8,9},{9,10},{10,11},{11... | collective-permute-start | bytes 393224 | tf_op jit(solution)/shard_map/while/body/eval_jaxpr/ppermute | solution.py:14
  252.9 4.7 %collective-permute-done = bf16[256,256]{1,0:T(8,128)(2,1)S(1)} collective-permute-done((bf16[256,256]{1,0:T(8,128)(2,1)S(1)}, bf16[256,256]{1,0:T(8,128)(2,1)S(1)}, u32[]{:S(2)}, u32[]{:S(2)}) %collective-permute-start) | collective-permute-done | bytes 131104 | tf_op jit(solution)/shard_map/while/body/eval_jaxpr/ppermute | solution.py:14
  257.7 5.5 %collective-permute-start = (bf16[256,256]{1,0:T(8,128)(2,1)S(1)}, bf16[256,256]{1,0:T(8,128)(2,1)S(1)}, u32[]{:S(2)}, u32[]{:S(2)}) collective-permute-start(bf16[256,256]{1,0:T(8,128)(2,1)S(1)} %get-tuple-element.278), channel_id=1, source_target_pairs={{0,1},{1,2},{2,3},{3,4},{4,5},{5,6},{6,7},{8,9},{9,10},{10,11},{11... | collective-permute-start | bytes 393224 | tf_op jit(solution)/shard_map/while/body/eval_jaxpr/ppermute | solution.py:14
  263.2 2.5 collective-permute-done
  265.7 5.9 %while.21 = (s32[]{:T(128)}, bf16[4,256,128]{1,2,0:T(8,128)(2,1)S(1)}, s32[256]{0:T(256)S(1)}, bf16[4,256,128]{2,1,0:T(8,128)(2,1)S(1)}, bf16[1280,256]{1,0:T(8,...) while((s32[]{:T(128)}, bf16[4,256,128]{1,2,0:T(8,128)(2,1)S(1)}, s32[256]{0:T(256)S(1)}, ...), condition=%wide.region_13.14_spmd.clone, body=%wide.region_10.13_spmd.clone.sunk | while | flops 171115520 | bytes 5002341 | solution.py:177
  265.7 0.5 fusion.84
  266.3 0.3 fusion.85
  266.6 0.4 fusion.86
  267.2 0.5 fusion.84
  267.7 0.3 fusion.85
  268.1 0.4 fusion.86
  268.7 0.5 fusion.84
  269.5 0.4 fusion.86
  270.1 0.5 fusion.84
  271.0 0.4 fusion.86
  271.6 49.3 %all-gather.11.cloned.1.call-done = bf16[512,8192]{1,0:T(8,128)(2,1)} async-done(((bf16[512,256]{1,0:T(8,128)(2,1)}), bf16[512,8192]{1,0:T(8,128)(2,1)}) %all-gather.11.cloned.1.call-update) | async-done | bytes 8388624 | tf_op jit(solution)/shard_map/all_gather | solution.py:180
  320.9 9.2 %fusion.19 = bf16[256,8192]{1,0:T(8,128)(2,1)} fusion(bf16[256,512]{0,1:T(8,128)(2,1)S(1)} %bitcast.73, bf16[512,8192]{1,0:T(8,128)(2,1)} %all-gather.11.cloned.1.call-done, bf16[256,8192]{1,0:T(8,128)(2,1)} %get-tuple-element.202), kind=kOutput, calls=%fused_computation.26 | convolution fusion | flops 2153775104 | bytes 17039360 | tf_op jit(solution)/shard_map/dot_general | solution.py:178
  (73 shorter events, 3.1 us)
Async XLA Ops:
  6.5 19.4 %copy-start = (bf16[1280,1280]{1,0:T(8,128)(2,1)S(1)}, bf16[1280,1280]{1,0:T(8,128)(2,1)}, u32[]{:S(2)}) copy-start(bf16[1280,1280]{1,0:T(8,128)(2,1)} %param.23) | copy-start | bytes 9830404
  6.5 66.8 %all-gather.5.cloned.1.call-start = ((), (), s32[]{:S(2)}) async-start(), calls=%async_computation.2 | async-start | bytes 1474560 | tf_op jit(solution)/shard_map/all_gather | solution.py:104
  7.8 12.6 %copy-start.4 = (s32[1,64]{1,0:T(1,128)S(1)}, s32[1,64]{1,0:T(1,128)}, u32[]{:S(2)}) copy-start(s32[1,64]{1,0:T(1,128)} %param.20) | copy-start | bytes 772
  13.6 12.4 %copy-start.2 = (bf16[64,1280]{1,0:T(8,128)(2,1)S(1)}, bf16[64,1280]{1,0:T(8,128)(2,1)}, u32[]{:S(2)}) copy-start(bf16[64,1280]{1,0:T(8,128)(2,1)} %param.19) | copy-start | bytes 491524
  21.8 5.9 %copy-start.3 = (f32[1280]{0:T(1024)S(1)}, f32[1280]{0:T(1024)}, u32[]{:S(2)}) copy-start(f32[1280]{0:T(1024)} %param.24) | copy-start | bytes 15364
  28.6 92.0 %all-gather.7.cloned.1.call-start = ((), (), s32[]{:S(2)}) async-start(), calls=%async_computation.3 | async-start | bytes 1474560 | tf_op jit(solution)/shard_map/all_gather | solution.py:111
  79.1 146.3 %all-gather.9.cloned.1.call-start = ((), (), s32[]{:S(2)}) async-start(), calls=%async_computation.4 | async-start | bytes 12976128 | tf_op jit(solution)/shard_map/all_gather | solution.py:138
  79.8 241.0 %all-gather.11.cloned.1.call-start = ((), (), s32[]{:S(2)}) async-start(), calls=%async_computation.5 | async-start | bytes 8650752 | tf_op jit(solution)/shard_map/all_gather | solution.py:180
  80.4 50.4 %copy-start.7 = (s32[16]{0:T(128)S(1)}, s32[16]{0:T(128)}, u32[]{:S(2)}) copy-start(s32[16]{0:T(128)} %param.27) | copy-start | bytes 196
  127.3 22.9 %copy-start.8 = (s32[1,4]{1,0:T(1,128)S(1)}, s32[1,4]{1,0:T(1,128)}, u32[]{:S(2)}) copy-start(s32[1,4]{1,0:T(1,128)} %param.30) | copy-start | bytes 52
  127.3 23.2 %copy-start.6 = (s32[256]{0:T(256)S(1)}, s32[256]{0:T(256)}, u32[]{:S(2)}) copy-start(s32[256]{0:T(256)} %param.29) | copy-start | bytes 3076
  127.3 17.4 %all-to-all-start = ((bf16[8,16,1024]{2,1,0:T(8,128)(2,1)}), bf16[8,16,1024]{2,1,0:T(8,128)(2,1)S(1)}, u32[]{:S(2)}, u32[]{:S(2)}) async-start(bf16[8,16,1024]{2,1,0:T(8,128)(2,1)} %bitcast.3), calls=%async_computation | async-start | bytes 524288 | tf_op jit(solution)/shard_map/all_to_all | solution.py:119
  146.5 29.3 %all-to-all-start.1 = ((bf16[8,4,8192]{2,1,0:T(4,128)(2,1)}), bf16[8,4,8192]{2,1,0:T(4,128)(2,1)S(1)}, u32[]{:S(2)}, u32[]{:S(2)}) async-start(bf16[8,4,8192]{2,1,0:T(4,128)(2,1)} %copy.46), calls=%async_computation.1 | async-start | bytes 1048576 | tf_op jit(solution)/shard_map/all_to_all | solution.py:127
  175.9 49.5 %copy-start.5 = (f32[8192]{0:T(1024)S(1)}, f32[8192]{0:T(1024)}, u32[]{:S(2)}) copy-start(f32[8192]{0:T(1024)} %param.31) | copy-start | bytes 98308
  234.9 6.5 %collective-permute-start = (bf16[256,256]{1,0:T(8,128)(2,1)S(1)}, bf16[256,256]{1,0:T(8,128)(2,1)S(1)}, u32[]{:S(2)}, u32[]{:S(2)}) collective-permute-start(bf16[256,256]{1,0:T(8,128)(2,1)S(1)} %get-tuple-element.278), channel_id=1, source_target_pairs={{0,1},{1,2},{2,3},{3,4},{4,5},{5,6},{6,7},{8,9},{9,10},{10,11},{11... | collective-permute-start | bytes 393224 | tf_op jit(solution)/shard_map/while/body/eval_jaxpr/ppermute | solution.py:14
  241.5 6.9 %collective-permute-start = (bf16[256,256]{1,0:T(8,128)(2,1)S(1)}, bf16[256,256]{1,0:T(8,128)(2,1)S(1)}, u32[]{:S(2)}, u32[]{:S(2)}) collective-permute-start(bf16[256,256]{1,0:T(8,128)(2,1)S(1)} %get-tuple-element.278), channel_id=1, source_target_pairs={{0,1},{1,2},{2,3},{3,4},{4,5},{5,6},{6,7},{8,9},{9,10},{10,11},{11... | collective-permute-start | bytes 393224 | tf_op jit(solution)/shard_map/while/body/eval_jaxpr/ppermute | solution.py:14
  248.4 9.2 %collective-permute-start = (bf16[256,256]{1,0:T(8,128)(2,1)S(1)}, bf16[256,256]{1,0:T(8,128)(2,1)S(1)}, u32[]{:S(2)}, u32[]{:S(2)}) collective-permute-start(bf16[256,256]{1,0:T(8,128)(2,1)S(1)} %get-tuple-element.278), channel_id=1, source_target_pairs={{0,1},{1,2},{2,3},{3,4},{4,5},{5,6},{6,7},{8,9},{9,10},{10,11},{11... | collective-permute-start | bytes 393224 | tf_op jit(solution)/shard_map/while/body/eval_jaxpr/ppermute | solution.py:14
  257.7 8.0 %collective-permute-start = (bf16[256,256]{1,0:T(8,128)(2,1)S(1)}, bf16[256,256]{1,0:T(8,128)(2,1)S(1)}, u32[]{:S(2)}, u32[]{:S(2)}) collective-permute-start(bf16[256,256]{1,0:T(8,128)(2,1)S(1)} %get-tuple-element.278), channel_id=1, source_target_pairs={{0,1},{1,2},{2,3},{3,4},{4,5},{5,6},{6,7},{8,9},{9,10},{10,11},{11... | collective-permute-start | bytes 393224 | tf_op jit(solution)/shard_map/while/body/eval_jaxpr/ppermute | solution.py:14
  320.9 9.2 %copy-start.1 = (bf16[1280,1280]{1,0:T(8,128)(2,1)S(1)}, bf16[1280,1280]{1,0:T(8,128)(2,1)}, u32[]{:S(2)}) copy-start(bf16[1280,1280]{1,0:T(8,128)(2,1)} %param.23) | copy-start | bytes 9830404
Sparse Core Ops, SparseCore 0:
  28.7 44.5 all-gather.4
  79.2 41.3 all-gather.6
  123.6 101.8 all-gather.8
  228.2 92.6 all-gather.10
where the time goes:
time: 337 us
  waiting for transfers between devices  232 us (69%)
  matrix products  49.9 us (15%)
  starting transfers between devices  25.1 us (7%)
  between operations  13.4 us (4%)
  local copies, waits for them, and re-layouts  12.6 us (4%)
  other arithmetic  3.41 us (1%)
    all_gather x1, waiting for transfers between devices, on_device(): lax.all_gather(attn_out, ('grp', 'seq'), axis=1, tiled=True)  49.3 us
    all_gather x1, waiting for transfers between devices, on_device(): lax.all_gather(attn_qkv, ('grp', 'seq'), axis=0, tiled=True)  44.7 us
    all_gather x1, waiting for transfers between devices, on_device(): lax.all_gather(merge_input, 'seq', axis=0, tiled=True)  44.6 us
    all_gather x1, waiting for transfers between devices, on_device(): lax.all_gather(hidden_part, 'seq', axis=1, tiled=True)  40.2 us
    all_to_all x1, waiting for transfers between devices, on_device(): lax.all_to_all(outgoing, 'seq', split_axis=0, concat_axis=0, tiled=True)  25.3 us
    ppermute x4, starting transfers between devices, from_behind(): lax.ppermute(value, axis, [(source, source + steps) for source in range(f...  17.7 us
    all_to_all x1, waiting for transfers between devices, on_device(): lax.all_to_all(column_part, 'seq', split_axis=0, concat_axis=1, tiled=True)  13.7 us
    ppermute x4, waiting for transfers between devices, from_behind(): lax.ppermute(value, axis, [(source, source + steps) for source in range(f...  12.8 us
  transfers between devices with their start and end apart: 10, of which 10 were waited for; matrix products, arithmetic and copies ran while one was open for 9% of the time, Pallas kernels for 0%

commit v1 on v0

--- a/solution.py
+++ b/solution.py
@@ -135,7 +135,12 @@
     normed = rms_scale(layer_in.astype(jnp.float32), attn_gain).astype(jnp.bfloat16)
     projected = jnp.dot(
         normed,
-        lax.all_gather(attn_qkv, ("grp", "seq"), axis=0, tiled=True),
+        jnp.concatenate(
+            lax.all_to_all(
+                jnp.stack([attn_qkv] * lax.axis_size(("grp", "seq"))), ("grp", "seq"), 0, 0
+            ),
+            axis=0,
+        ),
         preferred_element_type=jnp.float32,
     ).astype(jnp.bfloat16)
     query_width = attn_out.shape[0]

time: 337 us -> 554 us (1.64)
  waiting for transfers between devices: 232 us -> 427 us
  blocking collectives: 0 us -> 16.9 us
    all_to_all x1, waiting for transfers between devices: 25.3 us -> 322 us  [on_device(): lax.all_to_all(jnp.stack([attn_qkv] * lax.axis_size(('grp', 'seq'))), ('g...]
    all_gather x1, waiting for transfers between devices: 49.3 us -> 0.03 us  [on_device(): lax.all_gather(attn_out, ('grp', 'seq'), axis=1, tiled=True)]
    all_gather x1 -> x0, waiting for transfers between devices: 44.7 us -> none  [on_device(): lax.all_gather(attn_qkv, ('grp', 'seq'), axis=0, tiled=True)]
    all_to_all x0 -> x1, blocking collectives: none -> 16.9 us  [on_device(): lax.all_to_all(outgoing, 'seq', split_axis=0, concat_axis=0, tiled=True)]
    another operation x0 -> x1, local copies, waits for them, and re-layouts: none -> 5.88 us  [on_device(): jnp.stack([attn_qkv] * lax.axis_size(('grp', 'seq')))]
    all_to_all x1, waiting for transfers between devices: 13.7 us -> 7.95 us  [on_device(): lax.all_to_all(column_part, 'seq', split_axis=0, concat_axis=1, tiled=True)]
  transfers between devices with their start and end apart: 10 -> 9, of which waited for: 10 -> 8; matrix products, arithmetic and copies ran while one was open for 9% -> 4% of each run, Pallas kernels for 0% -> 0%
where the time goes in v1:
time: 554 us; the launch traced here: 552 us
  waiting for transfers between devices  427 us (77%)
  matrix products  49.8 us (9%)
  starting transfers between devices  22.1 us (4%)
  local copies, waits for them, and re-layouts  17.7 us (3%)
  blocking collectives  16.9 us (3%)
  between operations  15.1 us (3%)
    all_to_all x1, waiting for transfers between devices, on_device(): lax.all_to_all(jnp.stack([attn_qkv] * lax.axis_size(('grp', 'seq'))), ('g...  322 us
    all_gather x1, waiting for transfers between devices, on_device(): lax.all_gather(merge_input, 'seq', axis=0, tiled=True)  44.6 us
    all_gather x1, waiting for transfers between devices, on_device(): lax.all_gather(hidden_part, 'seq', axis=1, tiled=True)  41.5 us
    all_to_all x1, blocking collectives, on_device(): lax.all_to_all(outgoing, 'seq', split_axis=0, concat_axis=0, tiled=True)  16.9 us
    ppermute x4, starting transfers between devices, from_behind(): lax.ppermute(value, axis, [(source, source + steps) for source in range(f...  14.4 us
  transfers between devices with their start and end apart: 9, of which 8 were waited for; matrix products, arithmetic and copies ran while one was open for 4% of the time, Pallas kernels for 0%

profile of v1, /device:TPU:0, one launch (start us, length us, event | category | flops | bytes accessed | tf_op | source)
XLA Modules:
  0.0 552.5 jit_solution(17661107504658586684)
XLA Ops:
  7.4 1.2 fusion.36
  8.6 5.8 %convolution_convert_fusion.2 = bf16[64,3840]{1,0:T(8,128)(2,1)S(1)} fusion(bf16[1280,3840]{1,0:T(8,128)(2,1)} %param.22, bf16[64,1280]{1,0:T(8,128)(2,1)} %param.19, f32[1280]{0:T(1024)} %param.21, f32[64]{0:T(128)S(1)} %add_rsqrt_fusion.2), kind=kOutput, calls=%fused_computation.33 | convolution fusion | flops 629719040 | bytes 10491136 | tf_op jit(solution)/shard_map/while/body/eval_jaxpr/dot_general | solution.py:38
  14.4 0.8 fusion.63
  15.2 2.0 reshape.352
  17.2 2.0 reshape.351
  19.2 2.0 reshape.350
  21.3 1.3 fusion.64
  22.8 1.3 fusion.33
  24.0 0.9 copy.44
  24.9 1.9 convert_element_type.84
  26.8 1.7 multiply_reduce_fusion
  28.7 0.8 reshape.353
  29.5 44.6 %all-gather.4.cloned.1.call-done = bf16[128,5120]{1,0:T(8,128)(2,1)} async-done(((bf16[16,5120]{1,0:T(8,128)(2,1)}), bf16[128,5120]{1,0:T(8,128)(2,1)}) %all-gather.4.cloned.1.call-update) | async-done | bytes 1310736 | tf_op jit(solution)/shard_map/all_gather | solution.py:104
  74.2 5.8 %fusion.41 = bf16[128,640]{1,0:T(8,128)(2,1)} fusion(bf16[128,5120]{1,0:T(8,128)(2,1)} %all-gather.4.cloned.1.call-done, bf16[5120,640]{1,0:T(8,128)(2,1)} %param.25), kind=kOutput, calls=%fused_computation.56 | convolution fusion | flops 844185600 | bytes 8028160 | tf_op jit(solution)/shard_map/dot_general | solution.py:103
  80.0 41.5 %all-gather.6.cloned.1.call-done = bf16[128,5120]{1,0:T(8,128)(2,1)} async-done(((bf16[128,640]{1,0:T(8,128)(2,1)}), bf16[128,5120]{1,0:T(8,128)(2,1)}) %all-gather.6.cloned.1.call-update) | async-done | bytes 1310736 | tf_op jit(solution)/shard_map/all_gather | solution.py:111
  121.5 6.6 %convolution_convert_fusion.3 = bf16[128,1024]{1,0:T(8,128)(2,1)} fusion(bf16[128,5120]{1,0:T(8,128)(2,1)} %all-gather.6.cloned.1.call-done, bf16[5120,1024]{1,0:T(8,128)(2,1)} %param.26), kind=kOutput, calls=%fused_computation.44 | convolution fusion | flops 1342308352 | bytes 12058624 | tf_op jit(solution)/shard_map/dot_general | solution.py:110
  128.1 3.5 all-to-all-start
  131.9 8.0 %all-to-all-done = bf16[8,16,1024]{2,1,0:T(8,128)(2,1)S(1)} async-done(((bf16[8,16,1024]{2,1,0:T(8,128)(2,1)}), bf16[8,16,1024]{2,1,0:T(8,128)(2,1)S(1)}, u32[]{:S(2)}, u32[]{:S(2)}) %all-to-all-start) | async-done | bytes 262176 | tf_op jit(solution)/shard_map/all_to_all | solution.py:119
  140.4 0.4 copy.46
  140.8 16.9 %all_to_all.29 = bf16[8,4,8192]{2,1,0:T(4,128)(2,1)S(1)} all-to-all(bf16[8,4,8192]{2,1,0:T(4,128)(2,1)S(1)} %copy.46), channel_id=1, replica_groups=mesh['grp'=4,'seq'=8] {'seq'}, dimensions={0} | all-to-all | bytes 1048576 | tf_op jit(solution)/shard_map/all_to_all | solution.py:127
  157.7 5.9 %stack.2 = bf16[32,256,768]{2,1,0:T(8,128)(2,1)} broadcast(bf16[256,768]{1,0:T(8,128)(2,1)S(1)} %copy-done.3), dimensions={1,2} | broadcast | bytes 12976128 | tf_op jit(solution)/shard_map/stack | solution.py:140
  163.6 3.9 all-to-all-start.2
  168.5 4.8 fusion.21
  173.3 322.1 %all-to-all-done.2 = bf16[32,256,768]{2,1,0:T(8,128)(2,1)} async-done(((bf16[32,256,768]{2,1,0:T(8,128)(2,1)}), bf16[32,256,768]{2,1,0:T(8,128)(2,1)}, u32[]{:S(2)}, u32[]{:S(2)}) %all-to-all-start.2) | async-done | bytes 12582944 | tf_op jit(solution)/shard_map/all_to_all | solution.py:139
  495.4 9.3 %fusion.28 = bf16[256,768]{1,0:T(8,128)(2,1)S(1)} fusion(bf16[8192,768]{1,0:T(8,128)(2,1)} %bitcast.6, bf16[256,8192]{1,0:T(8,128)(2,1)} %get-tuple-element.202, f32[8192]{0:T(1024)S(1)} %copy-done.6, f32[256]{0:T(256)S(1)} %add_rsqrt_fusion), kind=kOutput, calls=%fused_computation.38 | convolution fusion | flops 3229810688 | bytes 17204224 | tf_op jit(solution)/shard_map/dot_general | solution.py:136
  504.9 25.0 %while.20 = (s32[]{:T(128)}, bf16[256,256]{1,0:T(8,128)(2,1)S(1)}, bf16[1280,256]{1,0:T(8,128)(2,1)S(1)}, s32[]{:T(128)}, s32[]{:T(128)}, /*index=5*/s32[]{:T(128)}, s32[]{:T(128)}, s32[]{:T(128)}) while((s32[]{:T(128)}, bf16[256,256]{1,0:T(8,128)(2,1)S(1)}, bf16[1280,256]{1,0:T(8,128)(2,1)S(1)}, s32[]{:T(128)}, s32[]{:T(128)}, ...), condition=%wide.region_9.10_spmd, body=%wide.region_8.9_spmd.sunk | while | flops 7 | bytes 1048763 | solution.py:167
  504.9 1.3 collective-permute-start
  506.2 2.9 collective-permute-done
  509.2 4.4 collective-permute-start
  513.6 2.5 collective-permute-done
  516.1 4.4 collective-permute-start
  520.5 2.5 collective-permute-done
  523.0 4.4 collective-permute-start
  527.4 2.5 collective-permute-done
  529.9 5.9 %while.21 = (s32[]{:T(128)}, bf16[4,256,128]{1,2,0:T(8,128)(2,1)S(1)}, s32[256]{0:T(256)S(1)}, bf16[4,256,128]{2,1,0:T(8,128)(2,1)S(1)}, bf16[1280,256]{1,0:T(8,...) while((s32[]{:T(128)}, bf16[4,256,128]{1,2,0:T(8,128)(2,1)S(1)}, s32[256]{0:T(256)S(1)}, ...), condition=%wide.region_13.14_spmd.clone, body=%wide.region_10.13_spmd.clone.sunk | while | flops 171115520 | bytes 5002349 | solution.py:182
  530.0 0.5 fusion.84
  530.5 0.3 fusion.85
  530.8 0.4 fusion.86
  531.4 0.5 fusion.84
  532.0 0.3 fusion.85
  532.3 0.4 fusion.86
  532.9 0.5 fusion.84
  533.4 0.3 fusion.85
  533.8 0.4 fusion.86
  534.4 0.5 fusion.84
  534.9 0.3 fusion.85
  535.2 0.4 fusion.86
  535.8 9.2 %fusion.19 = bf16[256,8192]{1,0:T(8,128)(2,1)} fusion(bf16[256,512]{0,1:T(8,128)(2,1)S(1)} %bitcast.74, bf16[512,8192]{1,0:T(8,128)(2,1)} %all-gather.8.cloned.1.call-done, bf16[256,8192]{1,0:T(8,128)(2,1)} %get-tuple-element.202), kind=kOutput, calls=%fused_computation.26 | convolution fusion | flops 2153775104 | bytes 17039360 | tf_op jit(solution)/shard_map/dot_general | solution.py:183
  (74 shorter events, 2.9 us)
Async XLA Ops:
  7.4 19.4 %copy-start = (bf16[1280,1280]{1,0:T(8,128)(2,1)S(1)}, bf16[1280,1280]{1,0:T(8,128)(2,1)}, u32[]{:S(2)}) copy-start(bf16[1280,1280]{1,0:T(8,128)(2,1)} %param.23) | copy-start | bytes 9830404
  7.4 66.8 %all-gather.4.cloned.1.call-start = ((), (), s32[]{:S(2)}) async-start(), calls=%async_computation.3 | async-start | bytes 1474560 | tf_op jit(solution)/shard_map/all_gather | solution.py:104
  8.6 12.6 %copy-start.5 = (s32[1,64]{1,0:T(1,128)S(1)}, s32[1,64]{1,0:T(1,128)}, u32[]{:S(2)}) copy-start(s32[1,64]{1,0:T(1,128)} %param.20) | copy-start | bytes 772
  14.4 12.4 %copy-start.2 = (bf16[64,1280]{1,0:T(8,128)(2,1)S(1)}, bf16[64,1280]{1,0:T(8,128)(2,1)}, u32[]{:S(2)}) copy-start(bf16[64,1280]{1,0:T(8,128)(2,1)} %param.19) | copy-start | bytes 491524
  22.6 5.9 %copy-start.4 = (f32[1280]{0:T(1024)S(1)}, f32[1280]{0:T(1024)}, u32[]{:S(2)}) copy-start(f32[1280]{0:T(1024)} %param.24) | copy-start | bytes 15364
  29.5 92.0 %all-gather.6.cloned.1.call-start = ((), (), s32[]{:S(2)}) async-start(), calls=%async_computation.4 | async-start | bytes 1474560 | tf_op jit(solution)/shard_map/all_gather | solution.py:111
  79.9 51.7 %copy-start.8 = (s32[16]{0:T(128)S(1)}, s32[16]{0:T(128)}, u32[]{:S(2)}) copy-start(s32[16]{0:T(128)} %param.27) | copy-start | bytes 196
  128.1 29.6 %copy-start.3 = (bf16[256,768]{1,0:T(8,128)(2,1)S(1)}, bf16[256,768]{1,0:T(8,128)(2,1)}, u32[]{:S(2)}) copy-start(bf16[256,768]{1,0:T(8,128)(2,1)} %param.32) | copy-start | bytes 1179652
  128.1 11.7 %all-to-all-start = ((bf16[8,16,1024]{2,1,0:T(8,128)(2,1)}), bf16[8,16,1024]{2,1,0:T(8,128)(2,1)S(1)}, u32[]{:S(2)}, u32[]{:S(2)}) async-start(bf16[8,16,1024]{2,1,0:T(8,128)(2,1)} %bitcast.3), calls=%async_computation | async-start | bytes 524288 | tf_op jit(solution)/shard_map/all_to_all | solution.py:119
  163.6 4.5 copy-start.9
  163.6 4.8 copy-start.7
  163.6 331.9 %all-to-all-start.2 = ((bf16[32,256,768]{2,1,0:T(8,128)(2,1)}), bf16[32,256,768]{2,1,0:T(8,128)(2,1)}, u32[]{:S(2)}, u32[]{:S(2)}) async-start(bf16[32,256,768]{2,1,0:T(8,128)(2,1)} %stack.2), calls=%async_computation.2 | async-start | bytes 25165824 | tf_op jit(solution)/shard_map/all_to_all | solution.py:139
  167.5 368.3 %all-gather.8.cloned.1.call-start = ((), (), s32[]{:S(2)}) async-start(), calls=%async_computation.5 | async-start | bytes 8650752 | tf_op jit(solution)/shard_map/all_gather | solution.py:185
  168.5 326.9 %copy-start.6 = (f32[8192]{0:T(1024)S(1)}, f32[8192]{0:T(1024)}, u32[]{:S(2)}) copy-start(f32[8192]{0:T(1024)} %param.31) | copy-start | bytes 98308
  504.9 4.2 collective-permute-start
  509.2 6.9 %collective-permute-start = (bf16[256,256]{1,0:T(8,128)(2,1)S(1)}, bf16[256,256]{1,0:T(8,128)(2,1)S(1)}, u32[]{:S(2)}, u32[]{:S(2)}) collective-permute-start(bf16[256,256]{1,0:T(8,128)(2,1)S(1)} %get-tuple-element.278), channel_id=1, source_target_pairs={{0,1},{1,2},{2,3},{3,4},{4,5},{5,6},{6,7},{8,9},{9,10},{10,11},{11... | collective-permute-start | bytes 393224 | tf_op jit(solution)/shard_map/while/body/eval_jaxpr/ppermute | solution.py:14
  516.1 6.9 %collective-permute-start = (bf16[256,256]{1,0:T(8,128)(2,1)S(1)}, bf16[256,256]{1,0:T(8,128)(2,1)S(1)}, u32[]{:S(2)}, u32[]{:S(2)}) collective-permute-start(bf16[256,256]{1,0:T(8,128)(2,1)S(1)} %get-tuple-element.278), channel_id=1, source_target_pairs={{0,1},{1,2},{2,3},{3,4},{4,5},{5,6},{6,7},{8,9},{9,10},{10,11},{11... | collective-permute-start | bytes 393224 | tf_op jit(solution)/shard_map/while/body/eval_jaxpr/ppermute | solution.py:14
  523.0 6.9 %collective-permute-start = (bf16[256,256]{1,0:T(8,128)(2,1)S(1)}, bf16[256,256]{1,0:T(8,128)(2,1)S(1)}, u32[]{:S(2)}, u32[]{:S(2)}) collective-permute-start(bf16[256,256]{1,0:T(8,128)(2,1)S(1)} %get-tuple-element.278), channel_id=1, source_target_pairs={{0,1},{1,2},{2,3},{3,4},{4,5},{5,6},{6,7},{8,9},{9,10},{10,11},{11... | collective-permute-start | bytes 393224 | tf_op jit(solution)/shard_map/while/body/eval_jaxpr/ppermute | solution.py:14
  535.8 9.2 %copy-start.1 = (bf16[1280,1280]{1,0:T(8,128)(2,1)S(1)}, bf16[1280,1280]{1,0:T(8,128)(2,1)}, u32[]{:S(2)}) copy-start(bf16[1280,1280]{1,0:T(8,128)(2,1)} %param.23) | copy-start | bytes 9830404
Sparse Core Ops, SparseCore 0:
  29.6 44.5 all-gather.3
  80.1 41.3 all-gather.5
Sparse Core Ops, SparseCore 1:
  170.8 276.9 all-gather.7
